TPU v7x, 128 devices: a whole 4x4x4 slice. The times are simulated.
128 devices in a mesh: train: 8 (over z, x_hi), serve: 16 (over x_lo, y, core).
Axes of the slice: x: 4 (x_hi: 2, x_lo: 2; x = x_hi * 2 + x_lo), y: 4, z: 4, core: 2. Of those that a mesh axis runs over, the one named last changes fastest.
Arguments:
- train_weights: bfloat16 [16, 7680, 2112], P(None, 'train', 'serve'), may hold values from -6 to 6
- row_offset: int32 [16, 9], replicated, may hold values from 0 to 7168, as said below
- block_group: int32 [16, 224, 1], P(None, 'train'), may hold values from 0 to 15; in each aligned block of 28 rows (0 to 27, 28 to 55, ..., all dimensions but the last counted through in order) at most 3 rows name the same one
Outputs:
- quant_codes: bfloat16 [16, 16, 8, 3, 32, 2112], P(None, 'serve', 'train')
- block_scales: float32 [16, 16, 8, 3, 2112], P(None, 'serve', 'train')
Inputs may be any that keep to these rules, and one draw needn't show every extreme that they name: For every layer l: row_offset[l, 0] = 0 and row_offset[l, 8] = 7168; every other row_offset[l, t] lies 1 to 32 rows above or below t * 896, never on it; in every layer one entry lies exactly 32 rows above and another exactly 32 rows below; layer 1 has the opposite sign of layer 0 at every such entry. `block_group`: within each aligned block of 28 entries (one training device's blocks of one layer), no group is named more than 3 times; some group reaches 3 in some of them.
All inputs are finite; a program needn't handle non-finite values.
Results may differ from a plain program's by a relative error of at most 0.001.
Values may be sent and summed in bfloat16 or wider, within the bound.
A program may use at most 128 MiB of HBM per device.

v0:
```python
import jax
import jax.numpy as jnp
from jax import lax
from jax.sharding import Mesh
from jax.sharding import PartitionSpec as P

BLOCK = 32
SHIFT = 32
SERVE = ("serve_0", "serve_1", "serve_2")


def padded_2(cells, sides, width):
    for axis, dim in sides:
        count = lax.axis_size(axis)
        ends = count - 1
        head = lax.slice_in_dim(cells, 0, width, axis=dim)
        tail = lax.slice_in_dim(cells, cells.shape[dim] - width, cells.shape[dim], axis=dim)
        cells = jnp.concatenate(
            [
                lax.ppermute(tail, axis, [(i, (i + 1) % count) for i in range(ends)]),
                cells,
                lax.ppermute(head, axis, [((i + 1) % count, i) for i in range(ends)]),
            ],
            axis=dim,
        )
    return cells


def cut_along(value, dim, peers):
    lengths = value.shape
    pieces = value.reshape(*lengths[:dim], peers, lengths[dim] // peers, *lengths[dim + 1 :])
    return jnp.moveaxis(pieces, dim, 0)


def joined_along(pieces, dim):
    lengths = list(pieces.shape[1:])
    lengths[dim] *= pieces.shape[0]
    return jnp.moveaxis(pieces, 0, dim).reshape(lengths)


def turned_blocks(pieces, axes, sequence):
    inside = pieces.shape[1:]
    out = pieces.reshape(*(lax.axis_size(a) for a in axes), *inside)
    for k in sequence:
        out = lax.all_to_all(out, axes[k], k, k, tiled=True)
    return out.reshape(-1, *inside)


def two_step_exchange(value, groups, sequence, split_dim, concat_dim):
    peers = lax.axis_size(groups[0]) * lax.axis_size(groups[1])
    pieces = cut_along(value, split_dim, peers)
    return joined_along(turned_blocks(pieces, groups, sequence), concat_dim)


def shards(train_weights, row_offset, block_group):
    train_n = lax.axis_size("train")
    serve_n = lax.axis_size(SERVE)
    train_idx = lax.axis_index("train")
    buffer_len = train_weights.shape[1]
    rows_dev = buffer_len - 2 * SHIFT
    blocks_dev = block_group.shape[1]
    slots_n = (blocks_dev + serve_n - 1) // serve_n + 1
    entries = jnp.arange(train_n + 1, dtype=jnp.int32)
    position = jnp.arange(blocks_dev, dtype=jnp.int32)
    earlier = position[None, :] < position[:, None]
    slot_range = jnp.arange(serve_n * slots_n, dtype=jnp.int32)
    group_ids = block_group[:, :, 0]
    layer_count = train_weights.shape[0]
    columns = train_weights.shape[2]
    first_row = (
        jnp.sum(jnp.where(entries[None, :] == train_idx, row_offset, 0), axis=1)
        - train_idx * rows_dev
    )
    next_row = (
        jnp.sum(jnp.where(entries[None, :] == train_idx + 1, row_offset, 0), axis=1)
        - train_idx * rows_dev
    )
    padded = padded_2(train_weights, (("train", 1),), SHIFT)
    left_rows = padded[:, :SHIFT]
    right_rows = padded[:, SHIFT + buffer_len :]
    own_rows = padded[:, 2 * SHIFT : 2 * SHIFT + rows_dev]
    filler = jnp.zeros((layer_count, rows_dev - SHIFT, columns), train_weights.dtype)
    left_full = jnp.concatenate([left_rows, filler], axis=1)
    right_full = jnp.concatenate([filler, right_rows], axis=1)
    row_pos = jnp.arange(rows_dev, dtype=jnp.int32)[None, :, None]
    joined = jnp.where(
        row_pos < first_row[:, None, None],
        left_full,
        jnp.where(row_pos >= next_row[:, None, None], right_full, own_rows),
    )
    blocks = joined.reshape(layer_count, blocks_dev, BLOCK, columns)
    same_group = group_ids[:, :, None] == group_ids[:, None, :]
    order_in = jnp.sum((same_group & earlier[None]).astype(jnp.int32), axis=2)
    slot_id = group_ids * slots_n + order_in
    onehot = slot_id[:, None, :] == slot_range[None, :, None]
    absmax = jnp.max(jnp.abs(blocks.astype(jnp.float32)), axis=2, keepdims=True)
    divisor = jnp.maximum(absmax, 0.25)
    coded = (blocks.astype(jnp.float32) / divisor).astype(jnp.bfloat16)
    codes_sent = jnp.einsum(
        "gqj,gjrc->gqrc", onehot.astype(jnp.bfloat16), coded, preferred_element_type=jnp.float32
    ).astype(jnp.bfloat16)
    codes_sent = codes_sent.reshape(layer_count, serve_n, slots_n, BLOCK, columns)
    scale_sent = jnp.einsum(
        "gqj,gjrc->gqrc", onehot.astype(jnp.float32), divisor, precision=lax.Precision.HIGHEST
    )
    scale_sent = scale_sent.reshape(layer_count, serve_n, slots_n, 1, columns)
    quant_codes = two_step_exchange(codes_sent, (("serve_0", "serve_1"), "serve_2"), (1, 0), 1, 4)
    block_scale = lax.all_to_all(scale_sent, SERVE, split_axis=1, concat_axis=4, tiled=True)
    return (
        quant_codes.reshape(layer_count, 1, 1, slots_n, BLOCK, -1),
        block_scale.reshape(layer_count, 1, 1, slots_n, -1),
    )


def solution(mesh):
    finer = Mesh(
        mesh.devices.reshape(mesh.shape["train"], 2, 4, 2),
        ("train", "serve_0", "serve_1", "serve_2"),
    )
    placed = (P(None, "train", SERVE), P(), P(None, "train", None))
    return jax.shard_map(
        shards,
        mesh=finer,
        in_specs=placed,
        out_specs=(P(None, SERVE, "train", None, None, None), P(None, SERVE, "train", None, None)),
        check_vma=False,
    )
```

profile of v0, /device:TPU:1, one launch (start us, length us, event | category | flops | bytes accessed | tf_op | source)
XLA Modules:
  0.0 289.9 jit_solution(9552514334235077035)
XLA Ops:
  0.6 0.0 copy-start.1
  0.6 0.0 copy-start
  0.6 1.5 fusion.12
  2.1 0.5 copy.83
  2.6 1.3 collective-permute-start.1
  3.9 0.5 copy.82
  4.4 6.1 %collective-permute-start = (bf16[16,32,132]{2,1,0:T(8,128)(2,1)S(1)}, bf16[16,32,132]{2,1,0:T(8,128)(2,1)S(1)}, u32[]{:S(2)}, u32[]{:S(2)}) collective-permute-start(bf16[16,32,132]{2,1,0:T(8,128)(2,1)S(1)} %copy.82), channel_id=1, source_target_pairs={{0,16},{16,32},{32,48},{48,64},{64,80},{80,96},{96,112},{1,17},{17... | collective-permute-start | bytes 405512 | tf_op jit(solution)/shard_map/ppermute | solution.py:20
  10.6 6.1 %slice.11 = bf16[16,896,132]{1,0,2:T(8,128)(2,1)} slice(bf16[16,960,132]{1,0,2:T(8,128)(2,1)} %param.3), slice={[0:16], [32:928], [0:132]} | slice | bytes 7569408 | tf_op jit(solution)/shard_map/slice | solution.py:81
  16.7 0.0 copy-done.1
  16.7 0.1 select_reduce_fusion.1
  16.9 0.1 iota_compare_fusion.2
  16.9 0.0 copy-done
  17.0 0.1 copy.61
  17.0 0.6 convert_reduce_fusion
  17.7 0.1 copy.63
  17.8 11.7 %copy.84 = bf16[16,896,132]{2,1,0:T(8,128)(2,1)} copy(bf16[16,896,132]{1,0,2:T(8,128)(2,1)} %slice.11) | data formatting | bytes 7569408
  29.5 0.1 iota_compare_fusion.3
  29.6 0.0 collective-permute-done.1
  29.6 0.0 collective-permute-done
  29.6 6.4 %select_select_fusion = bf16[16,896,132]{2,1,0:T(8,128)(2,1)S(1)} fusion(bf16[16,896,132]{2,1,0:T(8,128)(2,1)} %copy.84, bf16[16,32,132]{2,1,0:T(8,128)(2,1)S(1)} %collective-permute-done.1, bf16[16,32,132]{2,1,0:T(8,128)(2,1)S(1)} %collective-permute-done, pred[16,896]{1,0:T(8,128)(4,1)S(1)} %iota_compare_fusion.2, pred[16,896]{1,0:T(8,128)(4,1)S(1)} %iota_compare_fusion.3), kind=kLoop, calls=%fused_computation.6 | loop fusion | flops 3784704 | bytes 7868416 | tf_op jit(solution)/shard_map/jit(_where)/select_n | solution.py:86
  36.1 4.1 %fusion = f32[16,28,132]{2,1,0:T(8,128)S(1)} fusion(bf16[16,28,32,132]{3,2,1,0:T(8,128)(2,1)S(1)} %bitcast.35), kind=kLoop, calls=%fused_computation.2 | loop fusion | flops 5617920 | bytes 4021248 | tf_op jit(solution)/shard_map/reduce_max | solution.py:96
  40.2 0.8 broadcast_maximum_fusion
  41.0 7.3 %fusion.1 = bf16[16,28,32,132]{3,2,1,0:T(8,128)(2,1)} fusion(bf16[16,28,32,132]{3,2,1,0:T(8,128)(2,1)S(1)} %bitcast.36, f32[16,28,132]{2,1,0:T(8,128)} %broadcast_maximum_fusion), kind=kLoop, calls=%fused_computation.3 | loop fusion | flops 5677056 | bytes 7805952 | tf_op jit(solution)/shard_map/convert_element_type | solution.py:98
  48.3 0.7 fusion.7
  49.0 1.3 copy.73
  50.4 12.7 %fusion.4 = bf16[16,48,32,132]{3,1,2,0:T(8,128)(2,1)} fusion(bf16[16,28,32,132]{3,2,1,0:T(8,128)(2,1)} %fusion.1, s32[16,28]{1,0:T(8,128)S(1)} %copy.63), kind=kOutput, calls=%fused_computation.7 | convolution fusion | flops 184931328 | bytes 10274560 | tf_op jit(solution)/shard_map/gqj,gjrc->gqrc/dot_general | solution.py:99
  63.1 9.0 %copy.68 = bf16[16,48,32,132]{3,2,1,0:T(8,128)(2,1)S(1)} copy(bf16[16,48,32,132]{3,1,2,0:T(8,128)(2,1)} %fusion.4) | data formatting | bytes 12976128 | tf_op jit(solution)/shard_map/convert_element_type | solution.py:101
  72.1 1.9 copy.69
  74.0 16.4 %all_to_all.25 = bf16[8,2,16,1,3,32,132]{6,5,4,0,2,3,1:T(8,128)(2,1)} all-to-all(bf16[8,2,16,1,3,32,132]{6,5,4,0,2,3,1:T(8,128)(2,1)S(1)} %copy.69), channel_id=1, replica_groups=mesh['train'=8,'serve_0'=2,'serve_1'=4,'serve_2'=2] {'serve_2'}, dimensions={1} | all-to-all | bytes 12976128 | tf_op jit(solution)/shard_map/all_to_all | solution.py:45
  90.4 5.9 %all-to-all-start.2 = ((f32[16,16,3,1,132]{4,0,2,3,1:T(8,128)}), f32[16,16,3,1,132]{4,0,2,3,1:T(8,128)S(1)}, u32[]{:S(2)}, u32[]{:S(2)}) async-start(f32[16,16,3,1,132]{4,0,2,3,1:T(8,128)} %bitcast.13), calls=%async_computation.2 | async-start | bytes 1572864 | tf_op jit(solution)/shard_map/all_to_all | solution.py:108
  96.3 10.9 %copy.70 = bf16[8,2,16,1,3,32,132]{6,5,4,1,2,3,0:T(8,128)(2,1)} copy(bf16[8,2,16,1,3,32,132]{6,5,4,0,2,3,1:T(8,128)(2,1)} %all_to_all.25) | data formatting | bytes 12976128 | tf_op jit(solution)/shard_map/all_to_all | solution.py:45
  107.3 1.6 all-to-all-done.2
  108.9 5.4 %all-to-all-start.1 = ((bf16[8,2,16,1,3,32,132]{6,5,4,1,2,3,0:T(8,128)(2,1)}), bf16[8,2,16,1,3,32,132]{6,5,4,1,2,3,0:T(8,128)(2,1)}, u32[]{:S(2)}, u32[]{:S(2)}) async-start(bf16[8,2,16,1,3,32,132]{6,5,4,1,2,3,0:T(8,128)(2,1)} %copy.70), calls=%async_computation.1 | async-start | bytes 25165824 | tf_op jit(solution)/shard_map/all_to_all | solution.py:45
  114.3 0.5 copy.80
  114.7 1.9 reshape.118
  116.6 136.2 %all-to-all-done.1 = bf16[8,2,16,1,3,32,132]{6,5,4,1,2,3,0:T(8,128)(2,1)} async-done(((bf16[8,2,16,1,3,32,132]{6,5,4,1,2,3,0:T(8,128)(2,1)}), bf16[8,2,16,1,3,32,132]{6,5,4,1,2,3,0:T(8,128)(2,1)}, u32[]{:S(2)}, u32[]{:S(2)}) %all-to-all-start.1) | async-done | bytes 6488096 | tf_op jit(solution)/shard_map/all_to_all | solution.py:45
  252.8 6.3 %copy.71 = bf16[8,2,16,1,3,32,132]{6,5,4,2,1,0,3:T(8,128)(2,1)S(1)} copy(bf16[8,2,16,1,3,32,132]{6,5,4,1,2,3,0:T(8,128)(2,1)} %all-to-all-done.1) | data formatting | bytes 12976128 | tf_op jit(solution)/shard_map/all_to_all | solution.py:45
  259.1 9.7 %copy.72 = bf16[16,1,3,32,16,132]{5,4,3,2,0,1:T(8,128)(2,1)} copy(bf16[16,1,3,32,16,132]{5,3,2,0,4,1:T(8,128)(2,1)S(1)} %bitcast.38) | data formatting | bytes 12976128 | tf_op jit(solution)/shard_map/transpose | solution.py:38
  268.9 21.1 %reshape_reshape.7 = bf16[16,1,1,3,32,2112]{5,4,3,0,2,1:T(8,128)(2,1)} reshape(bf16[16,1,3,32,16,132]{5,4,3,2,0,1:T(8,128)(2,1)} %copy.72) | data formatting | bytes 12976128 | tf_op jit(solution)/shard_map/reshape;reshape | solution.py:110
  (5 shorter events, 0.0 us)
Async XLA Ops:
  0.6 16.1 %copy-start.1 = (s32[16,9]{1,0:T(8,128)S(1)}, s32[16,9]{1,0:T(8,128)}, u32[]{:S(2)}) copy-start(s32[16,9]{1,0:T(8,128)} %param.4) | copy-start | bytes 1732
  0.6 16.3 %copy-start = (s32[16,28,1]{1,2,0:T(1,128)S(1)}, s32[16,28,1]{1,2,0:T(1,128)}, u32[]{:S(2)}) copy-start(s32[16,28,1]{1,2,0:T(1,128)} %param.5) | copy-start | bytes 5380
  2.6 27.0 %collective-permute-start.1 = (bf16[16,32,132]{2,1,0:T(8,128)(2,1)S(1)}, bf16[16,32,132]{2,1,0:T(8,128)(2,1)S(1)}, u32[]{:S(2)}, u32[]{:S(2)}) collective-permute-start(bf16[16,32,132]{2,1,0:T(8,128)(2,1)S(1)} %copy.83), channel_id=1, source_target_pairs={{16,0},{32,16},{48,32},{64,48},{80,64},{96,80},{112,96},{17,1},{33... | collective-permute-start | bytes 405512 | tf_op jit(solution)/shard_map/ppermute | solution.py:22
  4.4 25.2 %collective-permute-start = (bf16[16,32,132]{2,1,0:T(8,128)(2,1)S(1)}, bf16[16,32,132]{2,1,0:T(8,128)(2,1)S(1)}, u32[]{:S(2)}, u32[]{:S(2)}) collective-permute-start(bf16[16,32,132]{2,1,0:T(8,128)(2,1)S(1)} %copy.82), channel_id=1, source_target_pairs={{0,16},{16,32},{32,48},{48,64},{64,80},{80,96},{96,112},{1,17},{17... | collective-permute-start | bytes 405512 | tf_op jit(solution)/shard_map/ppermute | solution.py:20
  90.4 18.5 %all-to-all-start.2 = ((f32[16,16,3,1,132]{4,0,2,3,1:T(8,128)}), f32[16,16,3,1,132]{4,0,2,3,1:T(8,128)S(1)}, u32[]{:S(2)}, u32[]{:S(2)}) async-start(f32[16,16,3,1,132]{4,0,2,3,1:T(8,128)} %bitcast.13), calls=%async_computation.2 | async-start | bytes 1572864 | tf_op jit(solution)/shard_map/all_to_all | solution.py:108
  108.9 143.9 %all-to-all-start.1 = ((bf16[8,2,16,1,3,32,132]{6,5,4,1,2,3,0:T(8,128)(2,1)}), bf16[8,2,16,1,3,32,132]{6,5,4,1,2,3,0:T(8,128)(2,1)}, u32[]{:S(2)}, u32[]{:S(2)}) async-start(bf16[8,2,16,1,3,32,132]{6,5,4,1,2,3,0:T(8,128)(2,1)} %copy.70), calls=%async_computation.1 | async-start | bytes 25165824 | tf_op jit(solution)/shard_map/all_to_all | solution.py:45
where the time goes:
time: 292 us; the launch traced here: 290 us
  waiting for transfers between devices  138 us (47%)
  local copies, waits for them, and re-layouts  83.2 us (28%)
  other arithmetic  19.6 us (7%)
  starting transfers between devices  18.7 us (6%)
  blocking collectives  16.4 us (6%)
  matrix products  13.4 us (5%)
    all_to_all x1, waiting for transfers between devices, turned_blocks(): out = lax.all_to_all(out, axes[k], k, k, tiled=True)  136 us
    another operation x1, local copies, waits for them, and re-layouts, shards(): quant_codes.reshape(layer_count, 1, 1, slots_n, BLOCK, -1)  21.1 us
    all_to_all x2, local copies, waits for them, and re-layouts, turned_blocks(): out = lax.all_to_all(out, axes[k], k, k, tiled=True)  17.2 us
    all_to_all x1, blocking collectives, turned_blocks(): out = lax.all_to_all(out, axes[k], k, k, tiled=True)  16.4 us
    unnamed x10, local copies, waits for them, and re-layouts  15.2 us
    dot_general x1, matrix products, shards(): jnp.einsum('gqj,gjrc->gqrc', onehot.astype(jnp.bfloat16), coded, preferre...  12.7 us
    transpose x1, local copies, waits for them, and re-layouts, joined_along(): return jnp.moveaxis(pieces, 0, dim).reshape(lengths)  9.73 us
    convert_element_type x1, local copies, waits for them, and re-layouts, shards(): codes_sent = jnp.einsum('gqj,gjrc->gqrc', onehot.astype(jnp.bfloat16), co...  9 us
  transfers between devices with their start and end apart: 4, of which 2 were waited for; matrix products, arithmetic and copies ran while one was open for 11% of the time, Pallas kernels for 0%

commit v1 on v0

v1 whole, which is shorter than its diff:
```python
import functools

import jax
import jax.numpy as jnp
from jax import lax
from jax.experimental import pallas as pl
from jax.experimental.pallas import tpu as pltpu
from jax.sharding import PartitionSpec as P

MESH = pl.DeviceIdType.MESH
BF = jnp.bfloat16
F32 = jnp.float32
LAYERS = 16
BLOCK = 32
BLOCKS_DEV = 28
ROWS_DEV = 896
COLS = 132
SERVE_N = 16
TRAIN_N = 8
SLOTS = 3
FEAT = SERVE_N * COLS
TILES = -(-FEAT // 128)
PARTS = (2, 4, 4, 4, 2)
FIRST = (0, 2, 6, 10, 14)
SIZES = tuple(n * SLOTS * BLOCK + 16 for n in PARTS)
BASES = tuple(sum(SIZES[:i]) for i in range(len(PARTS)))
TOTAL = sum(SIZES)
HALO = 16 + LAYERS * BLOCK
HALO_ENDS = tuple(16 + (f + n) * BLOCK for f, n in zip(FIRST, PARTS))
HALO_BASES = (0,) + HALO_ENDS[:-1]


def exchange(
    blocks_at, held, offsets, weights, out, scales,
    raw, edge, rot, lanes, tails, turned, rest, hsend, hrecv, send, recv, patch,
    raw_sem, edge_sem, hs_sem, hr_sem, s_sem, r_sem,
):
    t = lax.axis_index("train")
    me = lax.axis_index("serve")
    mx, my, mc = me // 8, lax.rem(me // 2, 4), lax.rem(me, 2)
    right, left = lax.rem(t + 1, TRAIN_N), lax.rem(t + TRAIN_N - 1, TRAIN_N)

    def peer(v):
        return (
            lax.rem(mx + v // 8, 2) * 8
            + lax.rem(my + lax.rem(v // 2, 4), 4) * 2
            + lax.rem(mc + lax.rem(v, 2), 2)
        )

    barrier = pltpu.get_barrier_semaphore()
    for v in range(1, SERVE_N):
        pl.semaphore_signal(barrier, inc=1, device_id={"serve": peer(v)}, device_id_type=MESH)
    for other in (left, right):
        pl.semaphore_signal(barrier, inc=1, device_id={"train": other}, device_id_type=MESH)

    edges = [
        pltpu.make_async_copy(weights.at[:, b], edge.at[side], edge_sem.at[side])
        for side, b in enumerate((BLOCKS_DEV + 1, 0))
    ]
    loads = [
        pltpu.make_async_copy(weights.at[pl.ds(f, n)], raw.at[pl.ds(f, n)], raw_sem.at[i])
        for i, (f, n) in enumerate(zip(FIRST, PARTS))
    ]
    for copy in edges + loads:
        copy.start()

    row = lax.broadcasted_iota(jnp.int32, (COLS, 256), 0)
    col = lax.broadcasted_iota(jnp.int32, (COLS, 256), 1)
    turn = (row < 128) & (col < 128) & (col == ((row + 4 * me) & 127))
    spread = (row >= 128) & (col >= 128) & ((col & 3) == row - 128)
    rot[...] = jnp.where(turn | spread, 1.0, 0.0).astype(BF)
    lane16 = lax.broadcasted_iota(jnp.int32, (16, 128), 1)
    for m in range(32):
        lanes[m] = jnp.where((lane16 >> 2) == m, 1.0, 0.0).astype(BF)
    rrow = lax.broadcasted_iota(jnp.int32, (128, 128), 0)
    rcol = lax.broadcasted_iota(jnp.int32, (128, 128), 1)
    patch[...] = jnp.where((rrow & 3) == (rcol & 3), 1.0, 0.0).astype(BF)

    for copy in edges:
        copy.wait()
    for side in range(2):
        def edge_step(i, total, side=side):
            x = edge[side, pl.ds(i * 4, 4)].reshape(4 * BLOCK, COLS)
            y = jnp.dot(x, rot[...], preferred_element_type=F32).astype(BF)
            hsend[side, pl.ds(pl.multiple_of(16 + i * 128, 16), 128)] = y[:, :128]
            for q in range(8):
                total = total + y[q * 16 : q * 16 + 16, 128:] * lanes[lax.rem(i * 8 + q + me, 32)]
            return total

        hsend[side, 0:16] = lax.fori_loop(0, LAYERS // 4, edge_step, jnp.zeros((16, 128), BF))

    pl.semaphore_wait(barrier, SERVE_N + 1)

    halos = []
    for i in range(len(PARTS)):
        window = pl.ds(HALO_BASES[i], HALO_ENDS[i] - HALO_BASES[i])
        for side, target in enumerate((right, left)):
            copy = pltpu.make_async_remote_copy(
                src_ref=hsend.at[side, window],
                dst_ref=hrecv.at[side, window],
                send_sem=hs_sem.at[side, i],
                recv_sem=hr_sem.at[side, i],
                device_id={"train": target},
                device_id_type=MESH,
            )
            copy.start()
            halos.append(copy)

    def block_copy(i, v):
        window = pl.ds(BASES[i], SIZES[i])
        return pltpu.make_async_remote_copy(
            src_ref=send.at[v, window],
            dst_ref=recv.at[me, window],
            send_sem=s_sem.at[i, v],
            recv_sem=r_sem.at[i, v],
            device_id={"serve": peer(v)},
            device_id_type=MESH,
        )

    block_row = lax.broadcasted_iota(jnp.int32, (BLOCK, 128), 0)

    for i, (f, n) in enumerate(zip(FIRST, PARTS)):
        loads[i].wait()

        def turn_step(j, carry, f=f):
            l, b = j // 7, lax.rem(j, 7) * 4
            x = raw[f + l, pl.ds(b + 1, 4)].reshape(4 * BLOCK, COLS)
            y = jnp.dot(x, rot[...], preferred_element_type=F32).astype(BF)
            turned[l, pl.ds(b, 4)] = y[:, :128].reshape(4, BLOCK, 128)
            rest[l, pl.ds(b, 4)] = y[:, 128:].reshape(4, BLOCK, 128)
            return carry

        lax.fori_loop(0, n * 7, turn_step, 0)
        halos[2 * i].wait_recv()
        halos[2 * i + 1].wait_recv()

        def patch_step(l, carry, f=f):
            layer = f + l
            first = offsets[layer, t] - t * ROWS_DEV
            last = offsets[layer, t + 1] - t * ROWS_DEV - (ROWS_DEV - BLOCK)
            for side, (b, take) in enumerate(
                ((0, block_row < first), (BLOCKS_DEV - 1, block_row >= last))
            ):
                main = hrecv[side, pl.ds(pl.multiple_of(16 + layer * BLOCK, 16), BLOCK)]
                packed = hrecv[side, 0:16]
                both = jnp.concatenate(
                    [packed * lanes[lax.rem(2 * layer + h + me, 32)] for h in range(2)], axis=0
                )
                tail = jnp.dot(both, patch[...], preferred_element_type=F32)
                turned[l, b] = jnp.where(take, main.astype(F32), turned[l, b].astype(F32)).astype(BF)
                rest[l, b] = jnp.where(take, tail, rest[l, b].astype(F32)).astype(BF)
            return carry

        lax.fori_loop(0, n, patch_step, 0)

        def fill(dest, index, group, i=i, f=f, n=n):
            total = jnp.zeros((16, 128), BF)
            for l in range(n):
                for k in range(SLOTS):
                    slot = l * SLOTS + k
                    b = blocks_at[f + l, group * SLOTS + k]
                    dest[index, pl.ds(BASES[i] + slot * BLOCK, BLOCK)] = turned[l, b]
                    pair = rest[l, b]
                    for h in range(2):
                        total = total + pair[h * 16 : h * 16 + 16] * lanes[
                            lax.rem(2 * slot + h + me, 32)
                        ]
            dest[index, pl.ds(BASES[i] + n * SLOTS * BLOCK, 16)] = total

        def send_step(j, carry, i=i, fill=fill):
            v = SERVE_N - 1 - j
            fill(send, v, peer(v))
            block_copy(i, v).start()
            return carry

        lax.fori_loop(0, SERVE_N - 1, send_step, 0)
        fill(recv, me, me)

    lane = lax.broadcasted_iota(jnp.int32, (BLOCK, 128), 1)
    for i, (f, n) in enumerate(zip(FIRST, PARTS)):
        def arrive(j, carry, i=i):
            block_copy(i, j + 1).wait_recv()
            return carry

        lax.fori_loop(0, SERVE_N - 1, arrive, 0)

        def tail_step(q, carry, i=i, n=n):
            total = jnp.zeros((16, 128), BF)
            for s in range(SERVE_N):
                total = total + recv[s, pl.ds(BASES[i] + n * SLOTS * BLOCK, 16)] * lanes[
                    lax.rem(q + s, 32)
                ]
            tails[q // 2, pl.ds(pl.multiple_of(lax.rem(q, 2) * 16, 16), 16)] = pltpu.roll(
                total.astype(F32), 128 - 4 * q, axis=1
            )
            return carry

        lax.fori_loop(0, 2 * n * SLOTS, tail_step, 0)

        def block_step(slot, carry, i=i, f=f):
            layer, k = f + slot // SLOTS, lax.rem(slot, SLOTS)
            there = held[layer, me * SLOTS + k].astype(F32)
            at = f * SLOTS + slot
            tail = tails[slot]
            before = None
            for j in range(TILES):
                if j < SERVE_N:
                    now = recv[j, pl.ds(pl.multiple_of(BASES[i] + slot * BLOCK, 16), BLOCK)].astype(F32)
                else:
                    now = tail
                if j == 0:
                    value = now
                else:
                    value = jnp.where(
                        lane < 4 * j - 4, before, jnp.where(lane < 4 * j, tail, now)
                    )
                before = now
                top = jnp.maximum(jnp.max(jnp.abs(value), axis=0, keepdims=True), 0.25)
                codes = (value * (there / top)).astype(BF)
                width = min(128, FEAT - j * 128)
                out[at, :, j * 128 : j * 128 + width] = codes[:, :width]
                scales[at, :, j * 128 : j * 128 + width] = (top * there)[:, :width]
            return carry

        lax.fori_loop(0, n * SLOTS, block_step, 0)

    for copy in halos:
        copy.wait_send()
    for i in range(len(PARTS)):
        def leave(j, carry, i=i):
            block_copy(i, j + 1).wait_send()
            return carry

        lax.fori_loop(0, SERVE_N - 1, leave, 0)


def shards(train_weights, row_offset, block_group):
    groups = block_group[:, :, 0]
    position = jnp.arange(BLOCKS_DEV, dtype=jnp.int32)
    earlier = position[None, :] < position[:, None]
    same = groups[:, :, None] == groups[:, None, :]
    order = jnp.sum((same & earlier[None]).astype(jnp.int32), axis=2)
    slot_id = groups * SLOTS + order
    onehot = slot_id[:, None, :] == jnp.arange(SERVE_N * SLOTS, dtype=jnp.int32)[None, :, None]
    blocks_at = jnp.sum(jnp.where(onehot, position[None, None, :], 0), axis=2)
    held = jnp.sum(onehot.astype(jnp.int32), axis=2)
    weights = train_weights.reshape(LAYERS, BLOCKS_DEV + 2, BLOCK, COLS)
    parts = len(PARTS)
    smem = pl.BlockSpec(memory_space=pltpu.SMEM)
    vmem = pl.BlockSpec(memory_space=pltpu.VMEM)
    codes, scales = pl.pallas_call(
        exchange,
        out_shape=(
            pltpu.VMEM((LAYERS * SLOTS, BLOCK, FEAT), BF),
            pltpu.VMEM((LAYERS * SLOTS, 1, FEAT), F32),
        ),
        in_specs=[smem, smem, smem, pl.BlockSpec(memory_space=pl.ANY)],
        out_specs=(vmem, vmem),
        scratch_shapes=[
            pltpu.VMEM((LAYERS, BLOCKS_DEV + 2, BLOCK, COLS), BF),
            pltpu.VMEM((2, LAYERS, BLOCK, COLS), BF),
            pltpu.VMEM((COLS, 256), BF),
            pltpu.VMEM((32, 16, 128), BF),
            pltpu.VMEM((max(PARTS) * SLOTS, BLOCK, 128), F32),
            pltpu.VMEM((max(PARTS), BLOCKS_DEV, BLOCK, 128), BF),
            pltpu.VMEM((max(PARTS), BLOCKS_DEV, BLOCK, 128), BF),
            pltpu.VMEM((2, HALO, 128), BF),
            pltpu.VMEM((2, HALO, 128), BF),
            pltpu.VMEM((SERVE_N, TOTAL, 128), BF),
            pltpu.VMEM((SERVE_N, TOTAL, 128), BF),
            pltpu.VMEM((128, 128), BF),
            pltpu.SemaphoreType.DMA((parts,)),
            pltpu.SemaphoreType.DMA((2,)),
            pltpu.SemaphoreType.DMA((2, parts)),
            pltpu.SemaphoreType.DMA((2, parts)),
            pltpu.SemaphoreType.DMA((parts, SERVE_N)),
            pltpu.SemaphoreType.DMA((parts, SERVE_N)),
        ],
        compiler_params=pltpu.CompilerParams(
            collective_id=1, has_side_effects=True, vmem_limit_bytes=44 * 2**20
        ),
    )(blocks_at, held, row_offset, weights)
    return (
        codes.reshape(LAYERS, 1, 1, SLOTS, BLOCK, FEAT),
        scales.reshape(LAYERS, 1, 1, SLOTS, FEAT),
    )


def solution(mesh):
    return jax.shard_map(
        shards,
        mesh=mesh,
        in_specs=(P(None, "train", "serve"), P(), P(None, "train", None)),
        out_specs=(P(None, "serve", "train", None, None, None), P(None, "serve", "train", None, None)),
        check_vma=False,
    )
```

time: 292 us -> 113 us (0.39)
  waiting for transfers between devices: 138 us -> 0 us
  Pallas kernels: 0 us -> 93.7 us
  local copies, waits for them, and re-layouts: 83.2 us -> 16.6 us
  starting transfers between devices: 18.7 us -> 0 us
  other arithmetic: 19.6 us -> 1.48 us
  blocking collectives: 16.4 us -> 0 us
  matrix products: 13.4 us -> 0 us
    all_to_all x2 -> x0, waiting for transfers between devices: 138 us -> none  [the longest x1 136 us: turned_blocks(): out = lax.all_to_all(out, axes[k], k, k, tiled=True)]
    pallas_call x0 -> x1, Pallas kernels: none -> 93.7 us  [shards(): pl.pallas_call(exchange, out_shape=(pltpu.VMEM((LAYERS * SLOTS, BLOCK, FE...]
    another operation x1 -> x0, local copies, waits for them, and re-layouts: 21.1 us -> none  [shards(): quant_codes.reshape(layer_count, 1, 1, slots_n, BLOCK, -1)]
    all_to_all x2 -> x0, local copies, waits for them, and re-layouts: 17.2 us -> none  [turned_blocks(): out = lax.all_to_all(out, axes[k], k, k, tiled=True)]
    all_to_all x1 -> x0, blocking collectives: 16.4 us -> none  [turned_blocks(): out = lax.all_to_all(out, axes[k], k, k, tiled=True)]
    dot_general x2 -> x0, matrix products: 13.4 us -> none  [the longest x1 12.7 us: shards(): jnp.einsum('gqj,gjrc->gqrc', onehot.astype(jnp.bfloat16), coded, preferre...]
    all_to_all x2 -> x0, starting transfers between devices: 11.3 us -> none  [the longest x1 5.9 us: shards(): lax.all_to_all(scale_sent, SERVE, split_axis=1, concat_axis=4, tiled=True)]
    transpose x1 -> x0, local copies, waits for them, and re-layouts: 9.73 us -> none  [joined_along(): return jnp.moveaxis(pieces, 0, dim).reshape(lengths)]
  transfers between devices with their start and end apart: 4 -> 0, of which waited for: 2 -> 0; matrix products, arithmetic and copies ran while one was open for 11% -> 0% of each run, Pallas kernels for 0% -> 0%
where the time goes in v1:
time: 113 us; the launch traced here: 112 us
  Pallas kernels  93.7 us (83%)
  local copies, waits for them, and re-layouts  16.6 us (15%)
  other arithmetic  1.48 us (1%)
    pallas_call x1, Pallas kernels, shards(): pl.pallas_call(exchange, out_shape=(pltpu.VMEM((LAYERS * SLOTS, BLOCK, FE...  93.7 us
    unnamed x6, local copies, waits for them, and re-layouts  16.6 us

profile of v1, /device:TPU:1, one launch (start us, length us, event | category | flops | bytes accessed | tf_op | source)
XLA Modules:
  0.0 112.4 jit_solution(6691880921710414551)
XLA Ops:
  0.6 0.0 copy-start
  0.7 0.8 copy.8
  1.4 1.3 %convert_reduce_fusion.1 = s32[16,28]{0,1:T(8,128)S(1)} fusion(s32[16,28]{1,0:T(8,128)} %bitcast.16, s32[16,28]{0,1:T(8,128)S(1)} %bitcast.15, pred[28,28]{1,0:T(8,128)(4,1)S(1)} %iota_compare_fusion.1), kind=kLoop, calls=%fused_computation.3 | loop fusion | flops 49728 | bytes 6160 | tf_op jit(solution)/shard_map/reduce_sum | solution.py:242
  2.8 0.1 convert_reduce_fusion
  2.9 12.2 %copy.10 = bf16[16,960,132]{2,1,0:T(8,128)(2,1)} copy(bf16[16,960,132]{1,0,2:T(8,128)(2,1)} %param.3) | data formatting | bytes 8110080 | tf_op args[0]
  15.2 0.0 copy-done
  15.2 93.7 %shard_map.50 = (bf16[48,32,2112]{2,1,0:T(8,128)(2,1)S(1)}, f32[48,1,2112]{2,1,0:T(1,128)S(1)}) custom-call(s32[16,48]{1,0:T(8,128)S(1)} %get-tuple-element.11.blocks_at, s32[16,48]{1,0:T(8,128)S(1)} %get-tuple-element.10.held, s32[16,9]{1,0:T(8,128)S(1)} %copy-done, bf16[16,30,32,132]{3,2,1,0:T(8,128)(2,1)} %bitcast.14), custom_call_target="tpu_custom_call" | custom-call | tf_op jit(solution)/shard_map/pallas_call | solution.py:251
  108.8 2.8 %copy.16 = bf16[16,1,1,3,32,2112]{5,4,3,2,1,0:T(8,128)(2,1)} copy(bf16[16,1,1,3,32,2112]{5,4,3,2,1,0:T(8,128)(2,1)S(1)} %bitcast.12) | data formatting | bytes 12976128
  111.7 0.8 copy.17
  (2 shorter events, 0.0 us)
Async XLA Ops:
  0.6 14.5 %copy-start = (s32[16,9]{1,0:T(8,128)S(1)}, s32[16,9]{1,0:T(8,128)}, u32[]{:S(2)}) copy-start(s32[16,9]{1,0:T(8,128)} %offsets.1) | copy-start | bytes 1732
